TPU v7x, 128 devices: a whole 4x4x4 slice. The times are simulated.
128 devices in a mesh: walk: 8 (over y, x_lo), orb: 16 (over x_hi, z, core).
Axes of the slice: x: 4 (x_hi: 2, x_lo: 2; x = x_hi * 2 + x_lo), y: 4, z: 4, core: 2. Of those that a mesh axis runs over, the one named last changes fastest.
Arguments:
- coefficients: bfloat16 [4096, 4096], P(None, 'orb'), may hold values from -6 to 6
- inverse: bfloat16 [8, 1024, 1024], P('walk', 'orb'), may hold values from -0.005859375 to 0.005859375
- cell_index: int32 [8, 3, 1024], P('walk'), may hold values from 0 to 15
- fraction: float32 [8, 3, 1024], P('walk'), may hold values from 0 to 1
- energies: float32 [8], P('walk'), may hold values from -8 to 8
- weights: float32 [8], P('walk'), may hold values from 0.5 to 2
- occupied: int32 [1024], replicated, may hold values from 0 to 4095, as said below
Outputs:
- gradient: float32 [1024, 4096], P('walk', 'orb')
Inputs may be any that keep to these rules, and one draw needn't show every extreme that they name: `occupied`: 1024 distinct orbital indices; every block of 256 consecutive orbital indices holds at most 96 of them, and some block holds exactly 96.
All inputs are finite; a program needn't handle non-finite values.
Results may differ from a plain program's by a relative error of at most 0.019.
Values may be sent and summed in bfloat16 or wider, within the bound.
A program may use at most 64 MiB of HBM per device.

v0:
```python
import jax
import jax.numpy as jnp
from jax import lax
from jax.sharding import PartitionSpec as P

GRID = 16


def joined_along(blocks, dim):
    dims = list(blocks.shape[1:])
    dims[dim] *= blocks.shape[0]
    return jnp.moveaxis(blocks, 0, dim).reshape(dims)


def work_in_pieces(shard, axis, dim, work, out_dim):
    span = shard.shape[dim]
    pieces = jnp.split(shard, 2, axis=dim) if span % 2 == 0 else [shard]
    first = jnp.arange(lax.axis_size(axis)) * span
    blocks = [lax.all_gather(slab, axis) for slab in pieces]
    made = [jax.vmap(work)(b, first + k * (span // len(pieces))) for k, b in enumerate(blocks)]
    return joined_along(jnp.concatenate(made, axis=out_dim + 1), out_dim)


def split_up(shard, dim, size):
    before, after = (shard.shape[:dim], shard.shape[dim + 1 :])
    return jnp.moveaxis(shard.reshape(*before, size, -1, *after), dim, 0)


def summed_on_arrival(shard, axis, dim):
    size = lax.axis_size(axis)
    blocks = lax.all_to_all(split_up(shard, dim, size), axis, 0, 0, tiled=True)
    return jnp.sum(blocks.astype(jnp.float32), axis=0)


def spline_basis(frac):
    remain = 1.0 - frac
    square = frac * frac
    cubed = square * frac
    values = (
        jnp.stack(
            [
                remain * remain * remain,
                3.0 * cubed - 6.0 * square + 4.0,
                -3.0 * cubed + 3.0 * square + 3.0 * frac + 1.0,
                cubed,
            ]
        )
        / 6.0
    )
    curves = jnp.stack([remain, 3.0 * frac - 2.0, 1.0 - 3.0 * frac, frac])
    return (values, curves)


def evaluate(coefficients, cell_one, frac_one, edge):
    shifts = jnp.arange(4, dtype=jnp.int32)[:, None] - 1
    index_x = (cell_one[0][None, :] + shifts) % edge
    index_y = (cell_one[1][None, :] + shifts) % edge
    index_z = (cell_one[2][None, :] + shifts) % edge
    value_x, curve_x = spline_basis(frac_one[0])
    value_y, curve_y = spline_basis(frac_one[1])
    value_z, curve_z = spline_basis(frac_one[2])
    plane = (index_y[:, None, :] * edge + index_z[None, :, :]).reshape(16, -1)
    value_yz = (value_y[:, None, :] * value_z[None, :, :]).reshape(16, -1)
    curve_yz = (
        curve_y[:, None, :] * value_z[None, :, :] + value_y[:, None, :] * curve_z[None, :, :]
    ).reshape(16, -1)
    electrons = cell_one.shape[1]
    orb_width = coefficients.shape[1]
    all_rows = (index_x[:, None, :] * (edge * edge) + plane[None, :, :]).reshape(64, electrons)
    weight_val = (value_x[:, None, :] * value_yz[None, :, :]).reshape(64, electrons)
    weight_lap = (
        curve_x[:, None, :] * value_yz[None, :, :] + value_x[:, None, :] * curve_yz[None, :, :]
    ).reshape(64, electrons)
    val_high = weight_val.astype(jnp.bfloat16)
    val_low = (weight_val - val_high.astype(jnp.float32)).astype(jnp.bfloat16)
    lap_high = weight_lap.astype(jnp.bfloat16)
    lap_low = (weight_lap - lap_high.astype(jnp.float32)).astype(jnp.bfloat16)
    stacked = jnp.stack([val_high, val_low, lap_high, lap_low])
    block = 256
    count = electrons // block
    rows_blocked = jnp.transpose(all_rows.reshape(64, count, block), (1, 2, 0))
    weights_blocked = jnp.transpose(stacked.reshape(4, 64, count, block), (2, 3, 0, 1))

    def one_block(items):
        rows_one, weights_one = items
        gathered = jnp.take(coefficients, rows_one, axis=0)
        parts = jnp.einsum(
            "nqk,nkw->nqw", weights_one, gathered, preferred_element_type=jnp.float32
        )
        orbital_sum = parts[:, 0, :] + parts[:, 1, :]
        laplace_sum = parts[:, 2, :] + parts[:, 3, :]
        return jnp.concatenate(
            [orbital_sum.astype(jnp.bfloat16), laplace_sum.astype(jnp.bfloat16)], axis=1
        )

    results = lax.map(one_block, (rows_blocked, weights_blocked))
    return results.reshape(electrons, 2 * orb_width)


def apply_inverse(inverse_rows, both_vals):

    def multiply(inv_piece, first_row):
        return jnp.dot(inv_piece, both_vals, preferred_element_type=jnp.float32)

    return work_in_pieces(inverse_rows, "orb", 0, multiply, 0)


def slot_tables(occupied, shard_index, orb_width, capacity):
    mine = occupied // orb_width == shard_index
    ranking = jnp.cumsum(mine.astype(jnp.int32)) - 1
    slot_ids = jnp.arange(capacity, dtype=jnp.int32)
    placed = mine[None, :] & (ranking[None, :] == slot_ids[:, None])
    positions = jnp.arange(occupied.shape[0], dtype=jnp.int32)
    slot_rows = jnp.sum(jnp.where(placed, positions[None, :], 0), axis=1)
    local_cols = occupied - shard_index * orb_width
    slot_cols = jnp.sum(jnp.where(placed, local_cols[None, :], 0), axis=1)
    filled = jnp.any(placed, axis=1)
    picker = (
        (jnp.arange(orb_width, dtype=jnp.int32)[:, None] == slot_cols[None, :]) & filled[None, :]
    ).astype(jnp.bfloat16)
    return (picker, slot_rows)


def couple_slots(kinetic_low, ratio, picker, slot_rows):
    slot_block = jnp.einsum(
        "ls,nl->sn", picker, kinetic_low, preferred_element_type=jnp.float32
    ).astype(jnp.bfloat16)
    ratio_rows = jnp.take(ratio, lax.all_gather(slot_rows, "orb", axis=0, tiled=True), axis=0)
    return jnp.einsum(
        "sn,sw->nw",
        lax.all_gather(slot_block, "orb", axis=0, tiled=True),
        ratio_rows,
        preferred_element_type=jnp.float32,
    )


def body(coefficients, inverse, cell_index, fraction, energies, weights, occupied):
    orb_width = coefficients.shape[1]
    orb_count = lax.axis_size("orb")
    shard_index = lax.axis_index("orb")
    electrons = occupied.shape[0]
    capacity = 3 * electrons // (2 * orb_count)
    picker, slot_rows = slot_tables(occupied, shard_index, orb_width, capacity)
    running = jnp.zeros((electrons, orb_width), jnp.float32)

    def finish(running, products, energy, weight):
        ratio = products[:, :orb_width].astype(jnp.bfloat16)
        kinetic = products[:, orb_width:]
        kinetic_low = kinetic.astype(jnp.bfloat16)
        coupled = couple_slots(kinetic_low, ratio, picker, slot_rows)
        sample_term = weight * (energy * ratio.astype(jnp.float32) - 0.5 * (kinetic - coupled))
        return running + sample_term

    def step_each(running, items):
        inverse_one, cells_one, frac_one, energy, weight = items
        products = apply_inverse(inverse_one, evaluate(coefficients, cells_one, frac_one, GRID))
        return (finish(running, products, energy, weight), None)

    running, unused = lax.scan(
        step_each, running, (inverse, cell_index, fraction, energies, weights)
    )
    return summed_on_arrival(running.astype(jnp.bfloat16), "walk", 0)


def solution(mesh):
    in_specs = (
        P(None, "orb"),
        P("walk", "orb", None),
        P("walk", None, None),
        P("walk", None, None),
        P("walk"),
        P("walk"),
        P(),
    )
    out_specs = P("walk", "orb")
    return jax.shard_map(body, mesh=mesh, in_specs=in_specs, out_specs=out_specs, check_vma=False)
```

profile of v0, /device:TPU:1, one launch (start us, length us, event | category | flops | bytes accessed | tf_op | source)
XLA Modules:
  0.0 392.3 jit_solution(9786935563459408953)
XLA Ops:
  6.5 1.7 fusion.39
  8.3 0.7 all-gather.4.cloned.1.call-update
  9.0 0.8 fusion.28
  9.8 0.8 broadcast_subtract_fusion.3
  10.9 0.1 add.378
  11.0 0.1 subtract_convert_fusion
  11.1 0.1 mul.535
  11.2 0.1 subtract_convert_fusion.1
  11.3 0.1 fusion.23
  11.5 0.1 add.399
  11.7 0.5 maximum_bitcast_fusion.1
  12.2 294.5 %while.17 = (s32[]{:T(128)}, bf16[4,256,512]{2,1,0:T(8,128)(2,1)}, bf16[4,256,4,64]{1,0,3,2:T(4,128)(2,1)S(1)}, s32[4,256,64]{1,0,2:T(4,128)S(1)}, bf16[4096,256]{1,0:T(8,128)(2,1)S(1)}, /*index=5*/s32[]{:T(128)}) while((s32[]{:T(128)}, bf16[4,256,512]{2,1,0:T(8,128)(2,1)}, bf16[4,256,4,64]{1,0,3,2:T(4,128)(2,1)S(1)}, ...), condition=%wide.region_1.2_spmd, body=%wide.region_0.1_spmd.sunk | while | flops 38699008 | bytes 30048844 | solution.py:96
  12.2 0.1 constant_dynamic-slice_fusion.4
  12.2 0.1 copy.28
  12.4 0.1 reshape.712
  12.5 64.8 %gather_fusion = bf16[16384,256]{1,0:T(8,128)(2,1)} fusion(bf16[4096,256]{1,0:T(8,128)(2,1)S(1)} %get-tuple-element.202, s32[16384]{0:T(1024)S(1)} %broadcast_clamp_fusion.2), kind=kCustom, calls=%fused_computation.clone.1 | custom fusion | bytes 16842752 | tf_op jit(solution)/shard_map/while/body/eval_jaxpr/while/body/eval_jaxpr/jit(_take)/gather | solution.py:86
  77.4 0.3 constant_dynamic-slice_fusion.5
  77.7 0.2 copy.29
  77.9 6.5 %fusion.53 = f32[256,4,256]{2,1,0:T(4,128)S(1)} fusion(bf16[256,64,256]{2,1,0:T(8,128)(2,1)} %bitcast.100, pred[256,64]{1,0:T(8,128)(4,1)S(1)} %compare_and_fusion.3, bf16[1,256,4,64]{3,2,1,0:T(4,128)(2,1)S(1)} %copy.29), kind=kOutput, calls=%fused_computation.2.clone.1 | convolution fusion | flops 37748736 | bytes 9584640 | tf_op jit(solution)/shard_map/while/body/eval_jaxpr/while/body/eval_jaxpr/nqk,nkw->nqw/dot_general | solution.py:87
  84.3 0.7 fusion.54
  85.1 0.7 fusion.55
  85.9 0.1 copy.28
  86.0 0.1 reshape.712
  86.1 64.8 %gather_fusion = bf16[16384,256]{1,0:T(8,128)(2,1)} fusion(bf16[4096,256]{1,0:T(8,128)(2,1)S(1)} %get-tuple-element.202, s32[16384]{0:T(1024)S(1)} %broadcast_clamp_fusion.2), kind=kCustom, calls=%fused_computation.clone.1 | custom fusion | bytes 16842752 | tf_op jit(solution)/shard_map/while/body/eval_jaxpr/while/body/eval_jaxpr/jit(_take)/gather | solution.py:86
  151.0 0.3 constant_dynamic-slice_fusion.5
  151.3 0.2 copy.29
  151.5 6.5 %fusion.53 = f32[256,4,256]{2,1,0:T(4,128)S(1)} fusion(bf16[256,64,256]{2,1,0:T(8,128)(2,1)} %bitcast.100, pred[256,64]{1,0:T(8,128)(4,1)S(1)} %compare_and_fusion.3, bf16[1,256,4,64]{3,2,1,0:T(4,128)(2,1)S(1)} %copy.29), kind=kOutput, calls=%fused_computation.2.clone.1 | convolution fusion | flops 37748736 | bytes 9584640 | tf_op jit(solution)/shard_map/while/body/eval_jaxpr/while/body/eval_jaxpr/nqk,nkw->nqw/dot_general | solution.py:87
  157.9 0.7 fusion.54
  158.7 0.7 fusion.55
  159.5 0.1 copy.28
  159.6 0.1 reshape.712
  159.7 64.8 %gather_fusion = bf16[16384,256]{1,0:T(8,128)(2,1)} fusion(bf16[4096,256]{1,0:T(8,128)(2,1)S(1)} %get-tuple-element.202, s32[16384]{0:T(1024)S(1)} %broadcast_clamp_fusion.2), kind=kCustom, calls=%fused_computation.clone.1 | custom fusion | bytes 16842752 | tf_op jit(solution)/shard_map/while/body/eval_jaxpr/while/body/eval_jaxpr/jit(_take)/gather | solution.py:86
  224.6 0.3 constant_dynamic-slice_fusion.5
  224.9 0.2 copy.29
  225.1 6.5 %fusion.53 = f32[256,4,256]{2,1,0:T(4,128)S(1)} fusion(bf16[256,64,256]{2,1,0:T(8,128)(2,1)} %bitcast.100, pred[256,64]{1,0:T(8,128)(4,1)S(1)} %compare_and_fusion.3, bf16[1,256,4,64]{3,2,1,0:T(4,128)(2,1)S(1)} %copy.29), kind=kOutput, calls=%fused_computation.2.clone.1 | convolution fusion | flops 37748736 | bytes 9584640 | tf_op jit(solution)/shard_map/while/body/eval_jaxpr/while/body/eval_jaxpr/nqk,nkw->nqw/dot_general | solution.py:87
  231.6 0.7 fusion.54
  232.3 0.7 fusion.55
  233.1 0.1 copy.28
  233.2 0.1 reshape.712
  233.3 64.8 %gather_fusion = bf16[16384,256]{1,0:T(8,128)(2,1)} fusion(bf16[4096,256]{1,0:T(8,128)(2,1)S(1)} %get-tuple-element.202, s32[16384]{0:T(1024)S(1)} %broadcast_clamp_fusion.2), kind=kCustom, calls=%fused_computation.clone.1 | custom fusion | bytes 16842752 | tf_op jit(solution)/shard_map/while/body/eval_jaxpr/while/body/eval_jaxpr/jit(_take)/gather | solution.py:86
  298.2 0.3 constant_dynamic-slice_fusion.5
  298.5 0.2 copy.29
  298.7 6.5 %fusion.53 = f32[256,4,256]{2,1,0:T(4,128)S(1)} fusion(bf16[256,64,256]{2,1,0:T(8,128)(2,1)} %bitcast.100, pred[256,64]{1,0:T(8,128)(4,1)S(1)} %compare_and_fusion.3, bf16[1,256,4,64]{3,2,1,0:T(4,128)(2,1)S(1)} %copy.29), kind=kOutput, calls=%fused_computation.2.clone.1 | convolution fusion | flops 37748736 | bytes 9584640 | tf_op jit(solution)/shard_map/while/body/eval_jaxpr/while/body/eval_jaxpr/nqk,nkw->nqw/dot_general | solution.py:87
  305.2 0.7 fusion.54
  305.9 0.7 fusion.55
  306.6 0.3 reduce-window.9
  306.9 0.1 slice.68
  307.0 0.1 slice_reduce_fusion
  307.2 0.1 add_bitcast_fusion
  307.2 0.2 fusion.17
  307.4 0.2 select_reduce_fusion
  307.6 2.2 convolution_bitcast_fusion
  309.9 2.2 convolution_bitcast_fusion.1
  312.2 0.2 pad_maximum_fusion
  312.4 1.3 convolution_convert_fusion
  315.0 0.6 dynamic-slice
  316.3 0.3 dynamic-update-slice
  316.5 13.7 %all-reduce = s32[1536]{0:T(1024)S(1)} all-reduce(s32[1536]{0:T(1024)S(1)} %dynamic-update-slice), channel_id=1, replica_groups=mesh['walk'=8,'orb'=16] {'orb'}, use_global_device_ids=true, to_apply=%add | all-reduce | flops 1536 | bytes 12288
  330.3 1.3 slice.118
  331.6 4.8 %gather_fusion.1 = bf16[1536,256]{1,0:T(8,128)(2,1)S(1)} fusion(bf16[1024,256]{1,0:T(8,128)(2,1)S(1)} %slice.118, s32[2048]{0:T(1024)S(1)} %pad_clamp_fusion), kind=kCustom, calls=%fused_computation.1 | custom fusion | bytes 1579008 | tf_op jit(solution)/shard_map/while/body/eval_jaxpr/jit(_take)/gather | solution.py:128
  336.3 31.8 %all-gather.8.cloned.1.call-done = bf16[1536,1024]{1,0:T(8,128)(2,1)} async-done(((bf16[96,1024]{1,0:T(8,128)(2,1)}), bf16[1536,1024]{1,0:T(8,128)(2,1)}) %all-gather.8.cloned.1.call-update) | async-done | bytes 3145744 | tf_op jit(solution)/shard_map/while/body/eval_jaxpr/all_gather | solution.py:131
  368.1 3.8 fusion.12
  371.9 13.2 %all_to_all.5 = bf16[8,128,256]{2,1,0:T(8,128)(2,1)S(1)} all-to-all(bf16[8,128,256]{2,1,0:T(8,128)(2,1)S(1)} %bitcast.105), channel_id=1, replica_groups=mesh['walk'=8,'orb'=16] {'walk'}, dimensions={0} | all-to-all | bytes 1048576 | tf_op jit(solution)/shard_map/all_to_all | solution.py:31
  385.0 0.7 convert_reduce_fusion
  (56 shorter events, 1.2 us)
Async XLA Ops:
  6.5 4.8 %copy-start.3 = (s32[1,3,1024]{2,0,1:T(1,128)S(1)}, s32[1,3,1024]{2,0,1:T(1,128)}, u32[]{:S(2)}) copy-start(s32[1,3,1024]{2,0,1:T(1,128)} %param.11) | copy-start | bytes 36868
  6.5 5.6 %copy-start = (bf16[4096,256]{1,0:T(8,128)(2,1)S(1)}, bf16[4096,256]{1,0:T(8,128)(2,1)}, u32[]{:S(2)}) copy-start(bf16[4096,256]{1,0:T(8,128)(2,1)} %param.9) | copy-start | bytes 6291460
  6.5 301.1 %all-gather.6.cloned.1.call-start = ((), (), s32[]{:S(2)}) async-start(), calls=%async_computation.2 | async-start | bytes 1114112 | tf_op jit(solution)/shard_map/while/body/eval_jaxpr/all_gather | solution.py:19
  8.2 301.7 %all-gather.4.cloned.1.call-start = ((), (), s32[]{:S(2)}) async-start(), calls=%async_computation.1 | async-start | bytes 1114112 | tf_op jit(solution)/shard_map/while/body/eval_jaxpr/all_gather | solution.py:19
  9.0 359.1 %all-gather.8.cloned.1.call-start = ((), (), s32[]{:S(2)}) async-start(), calls=%async_computation.3 | async-start | bytes 3342336 | tf_op jit(solution)/shard_map/while/body/eval_jaxpr/all_gather | solution.py:131
  12.2 294.5 %copy-start.2 = (s32[1024]{0:T(1024)S(1)}, s32[1024]{0:T(1024)}, u32[]{:S(2)}) copy-start(s32[1024]{0:T(1024)} %param.15) | copy-start | bytes 12292
  312.1 2.9 copy-start.4
  312.4 17.8 %copy-start.1 = (f32[16,64,512]{2,1,0:T(8,128)}, f32[16,64,512]{2,1,0:T(8,128)S(1)}, u32[]{:S(2)}) copy-start(f32[16,64,512]{2,1,0:T(8,128)S(1)} %pad_maximum_fusion) | copy-start | bytes 6291460
Sparse Core Ops, SparseCore 0:
  9.8 48.3 all-gather.5
  60.7 43.6 all-gather.3
  313.8 54.2 all-gather.7
where the time goes:
time: 393 us; the launch traced here: 392 us
  local copies, waits for them, and re-layouts  272 us (69%)
  matrix products  35.4 us (9%)
  waiting for transfers between devices  32.5 us (8%)
  blocking collectives  26.8 us (7%)
  between operations  15.4 us (4%)
  other arithmetic  10.2 us (3%)
    gather x4, local copies, waits for them, and re-layouts, one_block(): gathered = jnp.take(coefficients, rows_one, axis=0)  259 us
    all_gather x1, waiting for transfers between devices, couple_slots(): lax.all_gather(slot_block, 'orb', axis=0, tiled=True)  31.8 us
    dot_general x4, matrix products, one_block(): jnp.einsum('nqk,nkw->nqw', weights_one, gathered, preferred_element_type=...  25.9 us
    unnamed x1, blocking collectives  13.7 us
    all_to_all x1, blocking collectives, summed_on_arrival(): blocks = lax.all_to_all(split_up(shard, dim, size), axis, 0, 0, tiled=True)  13.2 us
  transfers between devices with their start and end apart: 3, of which 1 were waited for; matrix products, arithmetic and copies ran while one was open for 78% of the time, Pallas kernels for 0%

commit v1 on v0

v1 whole, which is shorter than its diff:
```python
import jax
import jax.numpy as jnp
from jax import lax
from jax.experimental import pallas as pl
from jax.experimental.pallas import tpu as pltpu
from jax.sharding import PartitionSpec as P

MESH = pl.DeviceIdType.MESH
GRID = 16
N = 1024
WIDE = 256
CAP = 96
ROWS = 64
PLANE = GRID * GRID
ETILE = 512
GROUP = 4
COPIES = 19

NT = (((1,), (1,)), ((), ()))


def dot_nt(left, right):
    return lax.dot_general(left, right, NT, preferred_element_type=jnp.float32)


def dot_nn(left, right):
    return jnp.dot(left, right, preferred_element_type=jnp.float32)


def axis_table(cell, frac):
    remain = 1.0 - frac
    square = frac * frac
    cubed = square * frac
    sixth = 1.0 / 6.0
    values = (
        remain * remain * remain * sixth,
        (3.0 * cubed - 6.0 * square + 4.0) * sixth,
        (-3.0 * cubed + 3.0 * square + 3.0 * frac + 1.0) * sixth,
        cubed * sixth,
    )
    curves = (remain, 3.0 * frac - 2.0, 1.0 - 3.0 * frac, frac)
    tap = (lax.broadcasted_iota(jnp.int32, (GRID, N), 0) - cell + (GRID + 1)) & (GRID - 1)
    value = jnp.zeros((GRID, N), jnp.float32)
    curve = jnp.zeros((GRID, N), jnp.float32)
    for a in range(4):
        hit = tap == a
        value = jnp.where(hit, values[a], value)
        curve = jnp.where(hit, curves[a], curve)
    return value, curve


def slots_of(occ):
    block = occ >> 8
    member = (lax.broadcasted_iota(jnp.int32, (16, N), 0) == block).astype(jnp.float32)
    tiles = [member[:, t * 128 : (t + 1) * 128] for t in range(N // 128)]
    stacked = jnp.concatenate(tiles, axis=0).astype(jnp.bfloat16)
    row = lax.broadcasted_iota(jnp.int32, (128, 256), 0)
    col = lax.broadcasted_iota(jnp.int32, (128, 256), 1)
    upper = jnp.where((row < col) | (col >= 128), 1.0, 0.0).astype(jnp.bfloat16)
    counted = dot_nn(stacked, upper)
    before = jnp.zeros((16, 128), jnp.float32)
    ranks = []
    for t in range(N // 128):
        piece = counted[t * 16 : (t + 1) * 16, :]
        ranks.append(jnp.sum(tiles[t] * (piece[:, :128] + before), axis=0, keepdims=True))
        before = before + piece[:, 128:]
    return block * CAP + jnp.concatenate(ranks, axis=1).astype(jnp.int32)


def one_hot_rows(first, count, which):
    rows = lax.broadcasted_iota(jnp.int32, (count, N), 0) + first
    return jnp.where(rows == which, 1.0, 0.0).astype(jnp.bfloat16)


class Gather:
    def __init__(self, own, buf, rows, send, recv, place):
        self.own, self.buf, self.rows, self.send, self.recv = own, buf, rows, send, recv
        self.xh, self.z, self.c = place
        self.started = []

    def block(self, dx, dz, dc, part=None):
        xh = 1 - self.xh if dx else self.xh
        c = 1 - self.c if dc else self.c
        z = (self.z + dz) % 4
        half = self.rows // 2
        size = self.rows if part is None else half
        first = (xh * 8 + z * 2 + c) * self.rows + (0 if part is None else part * half)
        return self.buf.at[pl.ds(pl.multiple_of(first, 16), size), :]

    def device(self, name):
        xh, z, c = self.xh, self.z, self.c
        if name == "zp":
            z = (z + 1) % 4
        if name == "zm":
            z = (z + 3) % 4
        if name == "x":
            xh = 1 - xh
        if name == "s":
            c = 1 - c
        return {"orb": xh * 8 + z * 2 + c}

    def push(self, src, dst, to, at):
        copy = pltpu.make_async_remote_copy(
            src_ref=src,
            dst_ref=dst,
            send_sem=self.send.at[at],
            recv_sem=self.recv.at[at],
            device_id=self.device(to),
            device_id_type=MESH,
        )
        copy.start()
        self.started.append(copy)

    def arrived(self, spot, frm, at):
        here = self.block(*spot)
        pltpu.make_async_remote_copy(
            src_ref=here,
            dst_ref=here,
            send_sem=self.send.at[at],
            recv_sem=self.recv.at[at],
            device_id=self.device(frm),
            device_id_type=MESH,
        ).wait_recv()
        return here

    def start_own(self):
        mine = self.block(0, 0, 0)
        for at, to in enumerate(("zp", "zm", "x", "s")):
            self.push(self.own, mine, to, at)

    def near_z(self):
        got = self.arrived((0, 3, 0), "zm", 0)
        half = self.block(0, 3, 0, 0)
        self.push(half, half, "zp", 4)
        self.push(got, got, "s", 10)
        got = self.arrived((0, 1, 0), "zp", 1)
        half = self.block(0, 1, 0, 1)
        self.push(half, half, "zm", 5)
        self.push(got, got, "s", 11)

    def near_x(self):
        got = self.arrived((1, 0, 0), "x", 2)
        self.push(got, got, "zp", 6)
        self.push(got, got, "zm", 7)
        self.push(got, got, "s", 12)

    def far_z(self):
        got = self.arrived((0, 2, 0, 0), "zm", 4)
        self.push(got, got, "x", 8)
        self.push(got, got, "s", 13)
        got = self.arrived((0, 2, 0, 1), "zp", 5)
        self.push(got, got, "x", 9)
        self.push(got, got, "s", 14)

    def cross(self):
        got = self.arrived((1, 3, 0), "zm", 6)
        self.push(got, got, "s", 15)
        got = self.arrived((1, 1, 0), "zp", 7)
        self.push(got, got, "s", 16)

    def far_cross(self):
        got = self.arrived((1, 2, 0, 0), "x", 8)
        self.push(got, got, "s", 17)
        got = self.arrived((1, 2, 0, 1), "x", 9)
        self.push(got, got, "s", 18)

    def from_partner(self):
        spots = {
            3: (0, 0, 1),
            10: (0, 3, 1),
            11: (0, 1, 1),
            12: (1, 0, 1),
            13: (0, 2, 1, 0),
            14: (0, 2, 1, 1),
            15: (1, 3, 1),
            16: (1, 1, 1),
            17: (1, 2, 1, 0),
            18: (1, 2, 1, 1),
        }
        for at, spot in spots.items():
            self.arrived(spot, "s", at)

    def drain(self):
        for copy in self.started:
            copy.wait_send()


def kernel(
    coef_hbm,
    inv_ref,
    cell_ref,
    frac_ref,
    energy_ref,
    weight_ref,
    occ_ref,
    out_ref,
    coef,
    coef_t,
    plane_val,
    plane_lap,
    x_val,
    x_lap,
    stage,
    lap_t,
    val_t,
    inv_all,
    occ_all,
    ratio_t,
    slot_t,
    y_t,
    outgoing,
    incoming,
    load_sem,
    inv_send,
    inv_recv,
    occ_send,
    occ_recv,
    red_send,
    red_recv,
):
    walk, orb = lax.axis_index("walk"), lax.axis_index("orb")
    yy, xl = walk // 2, walk % 2
    place = (orb // 8, (orb // 2) % 4, orb % 2)
    load = pltpu.make_async_copy(coef_hbm, coef, load_sem)
    load.start()
    inv_gather = Gather(inv_ref, inv_all, ROWS, inv_send, inv_recv, place)
    mine = occ_all.at[pl.ds(pl.multiple_of(orb * CAP, 16), CAP), :]
    occ_gather = Gather(mine, occ_all, CAP, occ_send, occ_recv, place)
    steps = ((2, 1), (2, 0), (1, 1), (1, 0), (3, 1), (3, 0), (0, 1))

    def walk_of(dy, dx):
        return ((yy + dy) % 4) * 2 + (1 - xl if dx else xl)

    barrier = pltpu.get_barrier_semaphore()
    for name in ("zp", "zm", "x", "s"):
        pl.semaphore_signal(
            barrier, inc=1, device_id=inv_gather.device(name), device_id_type=MESH
        )
    for dy, dx in steps:
        pl.semaphore_signal(
            barrier, inc=1, device_id={"walk": walk_of(dy, dx)}, device_id_type=MESH
        )
    pl.semaphore_wait(barrier, 4 + len(steps))
    inv_gather.start_own()

    bx, cx = axis_table(cell_ref[0:1, :], frac_ref[0:1, :])
    by, cy = axis_table(cell_ref[1:2, :], frac_ref[1:2, :])
    bz, cz = axis_table(cell_ref[2:3, :], frac_ref[2:3, :])
    x_val[...] = bx
    x_lap[...] = cx
    for y in range(GRID):
        rows = slice(y * GRID, (y + 1) * GRID)
        plane_val[rows, :] = by[y : y + 1, :] * bz
        plane_lap[rows, :] = cy[y : y + 1, :] * bz + by[y : y + 1, :] * cz
    inv_all[pl.ds(pl.multiple_of(orb * ROWS, 16), ROWS), :] = inv_ref[...]
    occ = occ_ref[...]
    slot = slots_of(occ)
    pick = dot_nt(one_hot_rows(orb * CAP, CAP, slot), one_hot_rows(orb * WIDE, WIDE, occ))
    pick = pick.astype(jnp.bfloat16)
    load.wait()
    for x in range(GRID):
        points = slice(x * PLANE, (x + 1) * PLANE)
        coef_t[:, points] = coef[points, :].T

    def spline(cols, lap):
        total = None
        for g in range(GRID // GROUP):
            for k in range(GROUP):
                x = g * GROUP + k
                if lap:
                    piece = (
                        x_lap[x : x + 1, cols] * plane_val[:, cols]
                        + x_val[x : x + 1, cols] * plane_lap[:, cols]
                    )
                else:
                    piece = x_val[x : x + 1, cols] * plane_val[:, cols]
                stage[g % 2, k * PLANE : (k + 1) * PLANE, :] = piece.astype(jnp.bfloat16)
            part = dot_nn(
                coef_t[:, g * GROUP * PLANE : (g + 1) * GROUP * PLANE], stage[g % 2]
            )
            total = part if total is None else total + part
        return total.astype(jnp.bfloat16)

    tiles = [slice(t * ETILE, (t + 1) * ETILE) for t in range(N // ETILE)]
    for cols in tiles:
        lap_t[:, cols] = spline(cols, True)
    mine[...] = dot_nn(pick, lap_t[...]).astype(jnp.bfloat16)
    inv_gather.near_z()
    occ_gather.start_own()
    inv_gather.near_x()
    val_t[:, tiles[0]] = spline(tiles[0], False)
    inv_gather.far_z()
    val_t[:, tiles[1]] = spline(tiles[1], False)
    inv_gather.cross()
    inv_gather.far_cross()
    occ_gather.near_z()
    occ_gather.near_x()
    inv_gather.from_partner()
    ratio_t[...] = dot_nt(val_t[...], inv_all[...]).astype(jnp.bfloat16)
    occ_gather.far_z()
    for t in range(3):
        hot = one_hot_rows(t * 512, 512, slot)
        slot_t[:, t * 512 : (t + 1) * 512] = dot_nt(ratio_t[...], hot).astype(jnp.bfloat16)
    occ_gather.cross()
    occ_gather.far_cross()
    occ_gather.from_partner()

    weight = weight_ref[0]
    scaled = weight * energy_ref[0]
    half = 0.5 * weight
    for cols in tiles:
        coupled = dot_nn(slot_t[...], occ_all[:, cols])
        y_t[:, cols] = (
            scaled * val_t[:, cols].astype(jnp.float32)
            + half * (coupled - lap_t[:, cols].astype(jnp.float32))
        ).astype(jnp.bfloat16)

    sends = []
    own = None
    for dy in (2, 1, 3, 0):
        first = pl.multiple_of(((yy + dy) % 4) * 256, 256)
        terms = dot_nt(inv_all[pl.ds(first, 256), :], y_t[...])
        outgoing[pl.ds(first, 256), :] = terms.astype(jnp.bfloat16)
        for dx in (1, 0):
            if (dy, dx) == (0, 0):
                own = jnp.where(xl == 0, terms[:128, :], terms[128:, :])
                continue
            at = steps.index((dy, dx))
            to = walk_of(dy, dx)
            copy = pltpu.make_async_remote_copy(
                src_ref=outgoing.at[pl.ds(pl.multiple_of(to * 128, 128), 128), :],
                dst_ref=incoming.at[at],
                send_sem=red_send.at[at],
                recv_sem=red_recv.at[at],
                device_id={"walk": to},
                device_id_type=MESH,
            )
            copy.start()
            sends.append(copy)
    inv_gather.drain()
    occ_gather.drain()
    total = own
    for copy, (dy, dx) in zip(sends[::-1], [s for s in steps][::-1]):
        at = steps.index((dy, dx))
        copy.wait()
        total = total + incoming[at].astype(jnp.float32)
    out_ref[...] = total


def body(coefficients, inverse, cell_index, fraction, energies, weights, occupied):
    vmem = pl.BlockSpec(memory_space=pltpu.VMEM)
    smem = pl.BlockSpec(memory_space=pltpu.SMEM)
    dma = pltpu.SemaphoreType.DMA
    return pl.pallas_call(
        kernel,
        out_shape=jax.ShapeDtypeStruct((128, WIDE), jnp.float32),
        in_specs=[pl.BlockSpec(memory_space=pl.ANY), vmem, vmem, vmem, smem, smem, vmem],
        out_specs=vmem,
        scratch_shapes=[
            pltpu.VMEM((GRID * PLANE, WIDE), jnp.bfloat16),
            pltpu.VMEM((WIDE, GRID * PLANE), jnp.bfloat16),
            pltpu.VMEM((PLANE, N), jnp.float32),
            pltpu.VMEM((PLANE, N), jnp.float32),
            pltpu.VMEM((GRID, N), jnp.float32),
            pltpu.VMEM((GRID, N), jnp.float32),
            pltpu.VMEM((2, GROUP * PLANE, ETILE), jnp.bfloat16),
            pltpu.VMEM((WIDE, N), jnp.bfloat16),
            pltpu.VMEM((WIDE, N), jnp.bfloat16),
            pltpu.VMEM((N, N), jnp.bfloat16),
            pltpu.VMEM((16 * CAP, N), jnp.bfloat16),
            pltpu.VMEM((WIDE, N), jnp.bfloat16),
            pltpu.VMEM((WIDE, 16 * CAP), jnp.bfloat16),
            pltpu.VMEM((WIDE, N), jnp.bfloat16),
            pltpu.VMEM((N, WIDE), jnp.bfloat16),
            pltpu.VMEM((7, 128, WIDE), jnp.bfloat16),
            dma,
            dma((COPIES,)),
            dma((COPIES,)),
            dma((COPIES,)),
            dma((COPIES,)),
            dma((7,)),
            dma((7,)),
        ],
        compiler_params=pltpu.CompilerParams(
            collective_id=0, has_side_effects=True, vmem_limit_bytes=60 * 1024 * 1024
        ),
        name="orbital_gradient",
    )(
        coefficients,
        inverse.reshape(ROWS, N),
        cell_index.reshape(3, N),
        fraction.reshape(3, N),
        energies,
        weights,
        occupied.reshape(1, N),
    )


def solution(mesh):
    in_specs = (
        P(None, "orb"),
        P("walk", "orb", None),
        P("walk", None, None),
        P("walk", None, None),
        P("walk"),
        P("walk"),
        P(),
    )
    out_specs = P("walk", "orb")
    return jax.shard_map(body, mesh=mesh, in_specs=in_specs, out_specs=out_specs, check_vma=False)
```

time: 393 us -> 51.3 us (0.13)
  local copies, waits for them, and re-layouts: 272 us -> 4.19 us
  Pallas kernels: 0 us -> 45.6 us
  matrix products: 35.4 us -> 0 us
  waiting for transfers between devices: 32.5 us -> 0 us
  blocking collectives: 26.8 us -> 0 us
  between operations: 15.4 us -> 1.31 us
  other arithmetic: 10.2 us -> 0 us
    gather x5 -> x0, local copies, waits for them, and re-layouts: 264 us -> none  [the longest x4 259 us: one_block(): gathered = jnp.take(coefficients, rows_one, axis=0)]
    pallas_call x0 -> x1, Pallas kernels: none -> 45.6 us  [body(): pl.pallas_call(kernel, out_shape=jax.ShapeDtypeStruct((128, WIDE), jnp.fl...]
    dot_general x8 -> x0, matrix products: 35.4 us -> none  [the longest x4 25.9 us: one_block(): jnp.einsum('nqk,nkw->nqw', weights_one, gathered, preferred_element_type=...]
    all_gather x3 -> x0, waiting for transfers between devices: 31.8 us -> none  [the longest x1 31.8 us: couple_slots(): lax.all_gather(slot_block, 'orb', axis=0, tiled=True)]
    unnamed x1 -> x0, blocking collectives: 13.7 us -> none
    all_to_all x1 -> x0, blocking collectives: 13.2 us -> none  [summed_on_arrival(): blocks = lax.all_to_all(split_up(shard, dim, size), axis, 0, 0, tiled=True)]
  transfers between devices with their start and end apart: 3 -> 0, of which waited for: 1 -> 0; matrix products, arithmetic and copies ran while one was open for 78% -> 0% of each run, Pallas kernels for 0% -> 0%
where the time goes in v1:
time: 51.3 us; the launch traced here: 51.1 us
  Pallas kernels  45.6 us (89%)
  local copies, waits for them, and re-layouts  4.19 us (8%)
  between operations  1.31 us (3%)
    pallas_call x1, Pallas kernels, body(): pl.pallas_call(kernel, out_shape=jax.ShapeDtypeStruct((128, WIDE), jnp.fl...  45.6 us
    unnamed x3, local copies, waits for them, and re-layouts  4.19 us

profile of v1, /device:TPU:1, one launch (start us, length us, event | category | flops | bytes accessed | tf_op | source)
XLA Modules:
  0.0 51.1 jit_solution(16892199934899360906)
XLA Ops:
  1.3 1.3 %copy.13 = s32[1,3,1024]{2,1,0:T(4,128)} copy(s32[1,3,1024]{2,0,1:T(1,128)} %param.9) | data formatting | bytes 24576
  2.6 1.3 %copy.12 = f32[1,3,1024]{2,1,0:T(4,128)} copy(f32[1,3,1024]{2,0,1:T(1,128)} %param.10) | data formatting | bytes 24576
  3.9 45.6 %orbital_gradient.1 = f32[128,256]{1,0:T(8,128)} custom-call(bf16[4096,256]{1,0:T(8,128)(2,1)} %coef_hbm.1, bf16[64,1024]{1,0:T(8,128)(2,1)} %bitcast.8, s32[3,1024]{1,0:T(4,128)} %bitcast.9, f32[3,1024]{1,0:T(4,128)} %bitcast.10, f32[1]{0:T(128)S(6)} %copy.15.energy_ref, f32[1]{0:T(128)S(6)} %copy.16.weight_ref, s32[1,1024]{1,0:T(1,128)} %bitcast.11), custom_call_target="tpu_custom_call" | custom-call | tf_op jit(solution)/shard_map/orbital_gradient/pallas_call | solution.py:354
  49.5 1.6 %copy.17 = f32[128,256]{1,0:T(8,128)} copy(f32[128,256]{1,0:T(8,128)} %orbital_gradient.1) | data formatting | bytes 262144

commit v2 on v1

v2 whole, which is shorter than its diff:
```python
import jax
import jax.numpy as jnp
from jax import lax
from jax.experimental import pallas as pl
from jax.experimental.pallas import tpu as pltpu
from jax.sharding import PartitionSpec as P

MESH = pl.DeviceIdType.MESH
GRID = 16
N = 1024
WIDE = 256
CAP = 96
ROWS = 64
PLANE = GRID * GRID
ETILE = 512
GROUP = 4
INV_PIECES = 2
OCC_PIECES = 2
ORDER = (
    ("i", "own", "zp", 0),
    ("i", "own", "zm", 1),
    ("i", "own", "zp", 1),
    ("i", "own", "x", 1),
    ("i", "own", "zm", 0),
    ("c", "tab", "", 0),
    ("i", "own", "x", 0),
    ("c", "L", "", 0),
    ("c", "L", "", 1),
    ("c", "L", "", 2),
    ("c", "L", "", 3),
    ("c", "L", "", 4),
    ("c", "L", "", 5),
    ("c", "L", "", 6),
    ("i", "got", "A", 0),
    ("c", "L", "", 7),
    ("i", "got", "B", 1),
    ("c", "mine", "", 0),
    ("o", "own", "zm", 1),
    ("o", "own", "x", 1),
    ("o", "own", "s", 0),
    ("o", "own", "zp", 0),
    ("c", "V", "", 0),
    ("c", "V", "", 1),
    ("c", "V", "", 2),
    ("i", "got", "X", 1),
    ("c", "V", "", 3),
    ("c", "V", "", 4),
    ("i", "got", "A", 1),
    ("i", "got", "X", 0),
    ("i", "got", "B", 0),
    ("i", "own", "s", 0),
    ("o", "own", "x", 0),
    ("c", "V", "", 5),
    ("i", "got", "C", 0),
    ("o", "got", "A", 0),
    ("i", "mate", "", 0),
    ("c", "V", "", 6),
    ("o", "got", "B", 1),
    ("c", "V", "", 7),
    ("i", "got", "D", 1),
    ("o", "own", "zp", 1),
    ("o", "mate", "", 0),
    ("i", "mate", "", 2),
    ("o", "own", "zm", 0),
    ("i", "got", "C", 1),
    ("i", "got", "E", 1),
    ("i", "mate", "", 3),
    ("o", "got", "X", 1),
    ("i", "mate", "", 4),
    ("o", "got", "X", 0),
    ("i", "got", "E", 0),
    ("o", "got", "C", 0),
    ("o", "got", "C", 1),
    ("o", "mate", "", 3),
    ("i", "got", "D", 0),
    ("i", "mate", "", 1),
    ("i", "got", "F", 1),
    ("o", "mate", "", 4),
    ("o", "got", "A", 1),
    ("i", "mate", "", 6),
    ("c", "R", "", 0),
    ("i", "got", "F", 0),
    ("c", "R", "", 1),
    ("o", "got", "B", 0),
    ("i", "mate", "", 5),
    ("o", "mate", "", 1),
    ("i", "mate", "", 7),
    ("c", "R", "", 2),
    ("c", "R", "", 3),
    ("o", "got", "D", 1),
    ("o", "got", "F", 0),
    ("c", "P", "", 0),
    ("o", "got", "E", 1),
    ("o", "got", "D", 0),
    ("o", "mate", "", 2),
    ("o", "got", "E", 0),
    ("c", "P", "", 1),
    ("o", "got", "F", 1),
    ("c", "P", "", 2),
    ("c", "P", "", 3),
    ("c", "Za", "", 0),
    ("o", "mate", "", 6),
    ("o", "mate", "", 5),
    ("o", "mate", "", 7),
    ("c", "Zb", "", 0),
)


NT = (((1,), (1,)), ((), ()))


def dot_nt(left, right):
    return lax.dot_general(left, right, NT, preferred_element_type=jnp.float32)


def dot_nn(left, right):
    return jnp.dot(left, right, preferred_element_type=jnp.float32)


def axis_table(cell, frac):
    remain = 1.0 - frac
    square = frac * frac
    cubed = square * frac
    sixth = 1.0 / 6.0
    values = (
        remain * remain * remain * sixth,
        (3.0 * cubed - 6.0 * square + 4.0) * sixth,
        (-3.0 * cubed + 3.0 * square + 3.0 * frac + 1.0) * sixth,
        cubed * sixth,
    )
    curves = (remain, 3.0 * frac - 2.0, 1.0 - 3.0 * frac, frac)
    tap = (lax.broadcasted_iota(jnp.int32, (GRID, N), 0) - cell + (GRID + 1)) & (GRID - 1)
    value = jnp.zeros((GRID, N), jnp.float32)
    curve = jnp.zeros((GRID, N), jnp.float32)
    for a in range(4):
        hit = tap == a
        value = jnp.where(hit, values[a], value)
        curve = jnp.where(hit, curves[a], curve)
    return value, curve


def slots_of(occ):
    block = occ >> 8
    member = (lax.broadcasted_iota(jnp.int32, (16, N), 0) == block).astype(jnp.float32)
    tiles = [member[:, t * 128 : (t + 1) * 128] for t in range(N // 128)]
    stacked = jnp.concatenate(tiles, axis=0).astype(jnp.bfloat16)
    row = lax.broadcasted_iota(jnp.int32, (128, 256), 0)
    col = lax.broadcasted_iota(jnp.int32, (128, 256), 1)
    upper = jnp.where((row < col) | (col >= 128), 1.0, 0.0).astype(jnp.bfloat16)
    counted = dot_nn(stacked, upper)
    before = jnp.zeros((16, 128), jnp.float32)
    ranks = []
    for t in range(N // 128):
        piece = counted[t * 16 : (t + 1) * 16, :]
        ranks.append(jnp.sum(tiles[t] * (piece[:, :128] + before), axis=0, keepdims=True))
        before = before + piece[:, 128:]
    return block * CAP + jnp.concatenate(ranks, axis=1).astype(jnp.int32)


def one_hot_rows(first, count, which):
    rows = lax.broadcasted_iota(jnp.int32, (count, N), 0) + first
    return jnp.where(rows == which, 1.0, 0.0).astype(jnp.bfloat16)


class Gather:
    KINDS = "ABXCDEF"
    SPOTS = {"O": (0, 0), "A": (0, 3), "B": (0, 1), "X": (1, 0), "C": (0, 2), "D": (1, 3), "E": (1, 1), "F": (1, 2)}

    def __init__(self, own, buf, rows, pieces, send, recv, place):
        self.own_ref, self.buf, self.rows, self.pieces = own, buf, rows, pieces
        self.send, self.recv = send, recv
        self.xh, self.z, self.c = place
        self.started = []
        self.seen = {}

    @staticmethod
    def copies(pieces):
        return 7 * pieces + 8

    def block(self, kind, piece=None, mate=0):
        dx, dz = self.SPOTS[kind]
        xh = 1 - self.xh if dx else self.xh
        c = 1 - self.c if mate else self.c
        z = (self.z + dz) % 4
        first = (xh * 8 + z * 2 + c) * self.rows
        size = self.rows
        if piece is not None:
            size = self.rows // self.pieces
            first = first + piece * size
        return self.buf.at[pl.ds(pl.multiple_of(first, 8), size), :]

    def device(self, name):
        xh, z, c = self.xh, self.z, self.c
        if name == "zp":
            z = (z + 1) % 4
        if name == "zm":
            z = (z + 3) % 4
        if name == "x":
            xh = 1 - xh
        if name == "s":
            c = 1 - c
        return {"orb": xh * 8 + z * 2 + c}

    def copy(self, src, dst, to, at):
        return pltpu.make_async_remote_copy(
            src_ref=src,
            dst_ref=dst,
            send_sem=self.send.at[at],
            recv_sem=self.recv.at[at],
            device_id=self.device(to),
            device_id_type=MESH,
        )

    def push(self, src, dst, to, at):
        copy = self.copy(src, dst, to, at)
        copy.start()
        self.started.append(copy)

    def index(self, kind, piece):
        return self.KINDS.index(kind) * self.pieces + piece

    def own(self, to, piece):
        if to == "s":
            self.push(self.own_ref, self.block("O"), "s", 7 * self.pieces)
            return
        size = self.rows // self.pieces
        src = self.own_ref.at[pl.ds(piece * size, size), :]
        kind = {"zp": "A", "zm": "B", "x": "X"}[to]
        self.push(src, self.block("O", piece), to, self.index(kind, piece))

    def got(self, kind, piece):
        here = self.block(kind, piece)
        frm = {"A": "zm", "B": "zp", "D": "zm", "E": "zp", "X": "x", "F": "x"}.get(kind)
        if frm is None:
            frm = "zm" if piece < self.pieces // 2 else "zp"
        self.copy(here, here, frm, self.index(kind, piece)).wait_recv()
        if kind == "A" and piece < self.pieces // 2:
            self.push(here, here, "zp", self.index("C", piece))
        if kind == "B" and piece >= self.pieces // 2:
            self.push(here, here, "zm", self.index("C", piece))
        if kind == "X":
            self.push(here, here, "zp", self.index("D", piece))
            self.push(here, here, "zm", self.index("E", piece))
        if kind == "C":
            self.push(here, here, "x", self.index("F", piece))
        self.seen[kind] = self.seen.get(kind, 0) + 1
        if self.seen[kind] == self.pieces:
            whole = self.block(kind)
            self.push(whole, whole, "s", 7 * self.pieces + 1 + self.KINDS.index(kind))

    def mate(self, _, which):
        here = self.block("OABXCDEF"[which], None, 1)
        self.copy(here, here, "s", 7 * self.pieces + which).wait_recv()

    def drain(self):
        for copy in self.started:
            copy.wait_send()


def kernel(
    coef_hbm,
    inv_hbm,
    cell_hbm,
    frac_hbm,
    energy_ref,
    weight_ref,
    occ_hbm,
    out_ref,
    coef,
    inv_ref,
    cell_ref,
    frac_ref,
    occ_ref,
    coef_t,
    plane_val,
    plane_lap,
    x_val,
    x_lap,
    stage,
    total,
    lap_t,
    val_t,
    inv_all,
    occ_all,
    ratio_t,
    slot_t,
    partial,
    y_t,
    outgoing,
    incoming,
    load_sem,
    inv_send,
    inv_recv,
    occ_send,
    occ_recv,
    red_send,
    red_recv,
):
    walk, orb = lax.axis_index("walk"), lax.axis_index("orb")
    yy, xl = walk // 2, walk % 2
    place = (orb // 8, (orb // 2) % 4, orb % 2)
    loads = []
    for at, (src, dst) in enumerate(
        (
            (inv_hbm, inv_ref),
            (cell_hbm, cell_ref),
            (frac_hbm, frac_ref),
            (occ_hbm, occ_ref),
            (coef_hbm, coef),
        )
    ):
        loads.append(pltpu.make_async_copy(src, dst, load_sem.at[at]))
        loads[-1].start()
    mine = occ_all.at[pl.ds(pl.multiple_of(orb * CAP, 16), CAP), :]
    gathers = {
        "i": Gather(inv_ref, inv_all, ROWS, INV_PIECES, inv_send, inv_recv, place),
        "o": Gather(mine, occ_all, CAP, OCC_PIECES, occ_send, occ_recv, place),
    }
    steps = ((2, 1), (2, 0), (1, 1), (1, 0), (3, 1), (3, 0), (0, 1))

    def walk_of(dy, dx):
        return ((yy + dy) % 4) * 2 + (1 - xl if dx else xl)

    barrier = pltpu.get_barrier_semaphore()
    for name in ("zp", "zm", "x", "s"):
        pl.semaphore_signal(
            barrier, inc=1, device_id=gathers["i"].device(name), device_id_type=MESH
        )
    for dy, dx in steps:
        pl.semaphore_signal(
            barrier, inc=1, device_id={"walk": walk_of(dy, dx)}, device_id_type=MESH
        )
    pl.semaphore_wait(barrier, 4 + len(steps))
    for load in loads[:4]:
        load.wait()

    weight = weight_ref[0]
    scaled = weight * energy_ref[0]
    half = 0.5 * weight
    kept = {}

    def tables():
        bx, cx = axis_table(cell_ref[0], frac_ref[0])
        by, cy = axis_table(cell_ref[1], frac_ref[1])
        bz, cz = axis_table(cell_ref[2], frac_ref[2])
        x_val[...] = bx
        x_lap[...] = cx
        for y in range(GRID):
            rows = slice(y * GRID, (y + 1) * GRID)
            plane_val[rows, :] = by[y : y + 1, :] * bz
            plane_lap[rows, :] = cy[y : y + 1, :] * bz + by[y : y + 1, :] * cz
        inv_all[pl.ds(pl.multiple_of(orb * ROWS, 16), ROWS), :] = inv_ref[...]
        loads[4].wait()
        for x in range(GRID):
            points = slice(x * PLANE, (x + 1) * PLANE)
            coef_t[:, points] = coef[points, :].T

    def spline(step, lap):
        t, g = step // (GRID // GROUP), step % (GRID // GROUP)
        cols = slice(t * ETILE, (t + 1) * ETILE)
        at = g % 2
        for k in range(GROUP):
            x = g * GROUP + k
            if lap:
                piece = (
                    x_lap[x : x + 1, cols] * plane_val[:, cols]
                    + x_val[x : x + 1, cols] * plane_lap[:, cols]
                )
            else:
                piece = x_val[x : x + 1, cols] * plane_val[:, cols]
            stage[at, k * PLANE : (k + 1) * PLANE, :] = piece.astype(jnp.bfloat16)
        part = dot_nn(coef_t[:, g * GROUP * PLANE : (g + 1) * GROUP * PLANE], stage[at])
        if g:
            part = part + total[...]
        if g == GRID // GROUP - 1:
            (lap_t if lap else val_t)[:, cols] = part.astype(jnp.bfloat16)
        else:
            total[...] = part

    def pick_occupied():
        occ = occ_ref[...]
        kept["slot"] = slots_of(occ)
        pick = dot_nt(
            one_hot_rows(orb * CAP, CAP, kept["slot"]), one_hot_rows(orb * WIDE, WIDE, occ)
        )
        mine[...] = dot_nn(pick.astype(jnp.bfloat16), lap_t[...]).astype(jnp.bfloat16)

    def side_of(far):
        return 1 - place[0] if far else place[0]

    def ratio_step(t):
        first = pl.multiple_of(side_of(t // 2) * 512 + (t % 2) * 256, 256)
        rows = pl.ds(first, 256)
        ratio_t[:, rows] = dot_nt(val_t[...], inv_all[rows, :]).astype(jnp.bfloat16)

    def slot_step(t):
        first = pl.multiple_of(side_of(t // 2) * 8 * CAP + (t % 2) * 4 * CAP, 4 * CAP)
        hot = one_hot_rows(first, 4 * CAP, kept["slot"])
        slot_t[:, pl.ds(first, 4 * CAP)] = dot_nt(ratio_t[...], hot).astype(jnp.bfloat16)

    def couple(far):
        spots = pl.ds(pl.multiple_of(side_of(far) * 8 * CAP, 8 * CAP), 8 * CAP)
        for cols in tiles:
            part = dot_nn(slot_t[:, spots], occ_all[spots, cols])
            if not far:
                partial[:, cols] = (
                    scaled * val_t[:, cols].astype(jnp.float32)
                    + half * (part - lap_t[:, cols].astype(jnp.float32))
                )
            else:
                y_t[:, cols] = (partial[:, cols] + half * part).astype(jnp.bfloat16)

    tiles = [slice(t * ETILE, (t + 1) * ETILE) for t in range(N // ETILE)]
    work = {
        "tab": lambda k: tables(),
        "L": lambda k: spline(k, True),
        "V": lambda k: spline(k, False),
        "mine": lambda k: pick_occupied(),
        "R": ratio_step,
        "P": slot_step,
        "Za": lambda k: couple(False),
        "Zb": lambda k: couple(True),
    }
    for what, name, kind, k in ORDER:
        if what == "c":
            work[name](k)
        else:
            getattr(gathers[what], name)(kind, k)

    sends = []
    own = None
    for pair in ((2, 1), (3, 0)):
        firsts = [pl.multiple_of(((yy + dy) % 4) * 256, 256) for dy in pair]
        terms = [dot_nt(inv_all[pl.ds(first, 256), :], y_t[...]) for first in firsts]
        for first, term in zip(firsts, terms):
            outgoing[pl.ds(first, 256), :] = term.astype(jnp.bfloat16)
        for dy, term in zip(pair, terms):
            for dx in (1, 0):
                if (dy, dx) == (0, 0):
                    own = jnp.where(xl == 0, term[:128, :], term[128:, :])
                    continue
                at = steps.index((dy, dx))
                to = walk_of(dy, dx)
                copy = pltpu.make_async_remote_copy(
                    src_ref=outgoing.at[pl.ds(pl.multiple_of(to * 128, 128), 128), :],
                    dst_ref=incoming.at[at],
                    send_sem=red_send.at[at],
                    recv_sem=red_recv.at[at],
                    device_id={"walk": to},
                    device_id_type=MESH,
                )
                copy.start()
                sends.append(copy)
    for gather in gathers.values():
        gather.drain()
    result = own
    for copy, (dy, dx) in zip(sends[::-1], [s for s in steps][::-1]):
        at = steps.index((dy, dx))
        copy.wait()
        result = result + incoming[at].astype(jnp.float32)
    out_ref[...] = result


def body(coefficients, inverse, cell_index, fraction, energies, weights, occupied):
    vmem = pl.BlockSpec(memory_space=pltpu.VMEM)
    smem = pl.BlockSpec(memory_space=pltpu.SMEM)
    hbm = pl.BlockSpec(memory_space=pl.ANY)
    dma = pltpu.SemaphoreType.DMA
    return pl.pallas_call(
        kernel,
        out_shape=jax.ShapeDtypeStruct((128, WIDE), jnp.float32),
        in_specs=[hbm, hbm, hbm, hbm, smem, smem, hbm],
        out_specs=vmem,
        scratch_shapes=[
            pltpu.VMEM((GRID * PLANE, WIDE), jnp.bfloat16),
            pltpu.VMEM((ROWS, N), jnp.bfloat16),
            pltpu.VMEM((3, 1, N), jnp.int32),
            pltpu.VMEM((3, 1, N), jnp.float32),
            pltpu.VMEM((1, N), jnp.int32),
            pltpu.VMEM((WIDE, GRID * PLANE), jnp.bfloat16),
            pltpu.VMEM((PLANE, N), jnp.float32),
            pltpu.VMEM((PLANE, N), jnp.float32),
            pltpu.VMEM((GRID, N), jnp.float32),
            pltpu.VMEM((GRID, N), jnp.float32),
            pltpu.VMEM((2, GROUP * PLANE, ETILE), jnp.bfloat16),
            pltpu.VMEM((WIDE, ETILE), jnp.float32),
            pltpu.VMEM((WIDE, N), jnp.bfloat16),
            pltpu.VMEM((WIDE, N), jnp.bfloat16),
            pltpu.VMEM((N, N), jnp.bfloat16),
            pltpu.VMEM((16 * CAP, N), jnp.bfloat16),
            pltpu.VMEM((WIDE, N), jnp.bfloat16),
            pltpu.VMEM((WIDE, 16 * CAP), jnp.bfloat16),
            pltpu.VMEM((WIDE, N), jnp.float32),
            pltpu.VMEM((WIDE, N), jnp.bfloat16),
            pltpu.VMEM((N, WIDE), jnp.bfloat16),
            pltpu.VMEM((7, 128, WIDE), jnp.bfloat16),
            dma((5,)),
            dma((Gather.copies(INV_PIECES),)),
            dma((Gather.copies(INV_PIECES),)),
            dma((Gather.copies(OCC_PIECES),)),
            dma((Gather.copies(OCC_PIECES),)),
            dma((7,)),
            dma((7,)),
        ],
        compiler_params=pltpu.CompilerParams(
            collective_id=0, has_side_effects=True, vmem_limit_bytes=60 * 1024 * 1024
        ),
        name="orbital_gradient",
    )(
        coefficients,
        inverse.reshape(ROWS, N),
        jnp.transpose(cell_index, (1, 0, 2)),
        jnp.transpose(fraction, (1, 0, 2)),
        energies,
        weights,
        occupied.reshape(1, N),
    )


def solution(mesh):
    in_specs = (
        P(None, "orb"),
        P("walk", "orb", None),
        P("walk", None, None),
        P("walk", None, None),
        P("walk"),
        P("walk"),
        P(),
    )
    out_specs = P("walk", "orb")
    return jax.shard_map(body, mesh=mesh, in_specs=in_specs, out_specs=out_specs, check_vma=False)
```

time: 51.3 us -> 43.7 us (0.85)
  Pallas kernels: 45.6 us -> 40.7 us
  local copies, waits for them, and re-layouts: 4.19 us -> 1.57 us
    pallas_call x1, Pallas kernels: 45.6 us -> 40.7 us  [body(): pl.pallas_call(kernel, out_shape=jax.ShapeDtypeStruct((128, WIDE), jnp.fl...]
    unnamed x3 -> x1, local copies, waits for them, and re-layouts: 4.19 us -> 1.57 us
where the time goes in v2:
time: 43.7 us; the launch traced here: 43.6 us
  Pallas kernels  40.7 us (93%)
  local copies, waits for them, and re-layouts  1.57 us (4%)
  between operations  1.3 us (3%)
    pallas_call x1, Pallas kernels, body(): pl.pallas_call(kernel, out_shape=jax.ShapeDtypeStruct((128, WIDE), jnp.fl...  40.7 us
    unnamed x1, local copies, waits for them, and re-layouts  1.57 us

profile of v2, /device:TPU:1, one launch (start us, length us, event | category | flops | bytes accessed | tf_op | source)
XLA Modules:
  0.0 43.6 jit_solution(9322664723273193489)
XLA Ops:
  1.3 40.7 %orbital_gradient.1 = f32[128,256]{1,0:T(8,128)} custom-call(bf16[4096,256]{1,0:T(8,128)(2,1)} %coef_hbm.1, bf16[64,1024]{1,0:T(8,128)(2,1)} %bitcast.4, s32[3,1,1024]{2,1,0:T(1,128)} %bitcast.5, f32[3,1,1024]{2,1,0:T(1,128)} %bitcast.6, f32[1]{0:T(128)S(6)} %copy.9.energy_ref, f32[1]{0:T(128)S(6)} %copy.10.weight_ref, s32[1,1024]{1,0:T(1,128)} %bitcast.7), custom_call_target="tpu_custom_call" | custom-call | tf_op jit(solution)/shard_map/orbital_gradient/pallas_call | solution.py:469
  42.0 1.6 %copy.11 = f32[128,256]{1,0:T(8,128)} copy(f32[128,256]{1,0:T(8,128)} %orbital_gradient.1) | data formatting | bytes 262144
